TPU v7x, 128 devices: a whole 4x4x4 slice. The times are simulated.
128 devices in a mesh: dp: 1, tp: 128 (over z, y, x, core).
Axes of the slice: x: 4, y: 4, z: 4, core: 2. Of those that a mesh axis runs over, the one named last changes fastest.
Arguments:
- hidden: bfloat16 [384, 3, 2048], P(('dp', 'tp'))
- w_head: bfloat16 [2048, 128256], P(None, 'tp')
- q_draft: float32 [384, 2, 128256], P(('dp', 'tp'))
- draft_tok: int32 [384, 2], P('dp')
Outputs:
- output 1: float32 [384, 2], P('dp')
- output 2: float32 [384], P('dp')
- output 3: float32 [384, 2, 128256], P('dp', None, 'tp')
- output 4: float32 [384, 128256], P('dp', 'tp')
All inputs are finite; a program needn't handle non-finite values.
Results may differ from a plain program's by a relative error of at most 0.001.
Values are sent between devices in bfloat16 or wider.
A program may use at most 1 GiB of HBM per device.

v0:
```python
import functools

import jax
import jax.numpy as jnp
from jax import lax
from jax.experimental import pallas as pl
from jax.experimental.layout import Layout, with_layout_constraint
from jax.experimental.pallas import tpu as pltpu
from jax.sharding import PartitionSpec as P

INV_TEMP = 1.25
DEV = 128
SEQ = 3
NPOS = 3
DRAFT = 2
BATCH = 384
DIM = 2048
VOCAB = 128256
SHARD = VOCAB // DEV
LANES = 128
TILES = VOCAB // LANES
CHUNKS = 8
TAIL = SHARD - (CHUNKS - 1) * LANES
ROWS_P = 1008
TAIL_P = ROWS_P - (CHUNKS - 1) * LANES
KC = DIM // LANES
HROWS = SEQ * NPOS * KC
COLS = NPOS * BATCH
COLS_P = 1280
CT = COLS // LANES
BT = BATCH // LANES
BLK = SEQ * CHUNKS
PITCH = 49
NEG = -1e30
STAT = 18
MESH = pl.DeviceIdType.MESH


def remote(src, dst, ssem, rsem, dev):
    return pltpu.make_async_remote_copy(
        src_ref=src, dst_ref=dst, send_sem=ssem, recv_sem=rsem,
        device_id={'tp': dev}, device_id_type=MESH)


def reduce_stage(buf, slot, count, ssem, rsem, device, payload):
    buf.reshape(count * STAT, LANES)[pl.ds(slot * STAT, STAT), :] = payload
    here = buf.at[pl.ds(slot * STAT, STAT)]
    for r in range(1, count):
        remote(here, here, ssem, rsem, device((slot + r) % count)).start()


def wait_rows(ref, rows, sem):
    part = ref.at[pl.ds(0, rows)]
    pltpu.make_async_copy(part, part, sem).wait()


def finish(buf, count, rsem):
    wait_rows(buf, (count - 1) * STAT, rsem)
    rows = buf.reshape(count * STAT, LANES)
    return [rows[k * STAT:(k + 1) * STAT, :] for k in range(count)]


def merge_max_sum(parts):
    m = parts[0][0:CT]
    for p in parts[1:]:
        m = jnp.maximum(m, p[0:CT])
    s = parts[0][CT:2 * CT] * jnp.exp(parts[0][0:CT] - m)
    for p in parts[1:]:
        s = s + p[CT:2 * CT] * jnp.exp(p[0:CT] - m)
    return jnp.concatenate([m, s], axis=0)


def merge_add(parts):
    total = parts[0]
    for p in parts[1:]:
        total = total + p
    return total


def kernel(q_hbm, w_hbm, h_hbm, tok_hbm,
           ex_hbm, bo_hbm, out_ref,
           tok_ref, qbuf, wbuf, hloc, hidb, bounce, hmat, z, send, recv, exbuf, stat, peak, scale,
           a1, b1, a2, b2,
           lsem, ag_s, ag_r, ag_r2, d2d_s, d2d_r, qs, qr_sem, rs, rr):
    scope = jax.named_scope
    me = lax.axis_index('tp')
    core = me % 2
    coord = (me // 32, (me // 8) % 4, (me // 2) % 4)
    unit = (32, 8, 2)
    partner = me + 1 - 2 * core
    hop = [[((coord[d] + r) % 4) * unit[d] for r in range(4)] for d in range(3)]

    def device(rz, ry, rx, rc):
        return hop[0][rz] + hop[1][ry] + hop[2][rx] + (core if rc == 0 else 1 - core)

    hcp = pltpu.make_async_copy(h_hbm, hloc, lsem.at[2])
    hcp.start()
    qcp = pltpu.make_async_copy(q_hbm, qbuf.at[pl.ds(0, SEQ * TILES * DRAFT)], lsem.at[0])
    qcp.start()
    wcp = pltpu.make_async_copy(w_hbm, wbuf, lsem.at[1])
    wcp.start()
    tcp = pltpu.make_async_copy(tok_hbm, tok_ref, lsem.at[3])
    tcp.start()
    barrier = pltpu.get_barrier_semaphore()
    peers = [partner]
    for d in range(3):
        for r in range(1, 4):
            steps = [0, 0, 0]
            steps[d] = r
            peers.append(device(*steps, 0))
    for dev in peers:
        pl.semaphore_signal(barrier, inc=1, device_id={'tp': dev}, device_id_type=MESH)

    with scope('hid'):
        hcp.wait()
        for s in range(SEQ):
            x = hloc[s].astype(jnp.float32)
            for kc in range(KC):
                bounce[pl.ds(s * 48 + kc, NPOS, stride=KC), :] = x[:, kc * LANES:(kc + 1) * LANES]
        hidb[pl.ds(pl.multiple_of(me * HROWS, 16), HROWS), :] = bounce[0:HROWS, :].astype(jnp.bfloat16)
    with scope('barrier'):
        pl.semaphore_wait(barrier, len(peers))

    hview = hidb.reshape(4, 4, 4, 2, SEQ, HROWS // SEQ, LANES)

    def ag_phase(phase):
        for j in range(3):
            order = [(j + k) % 3 for k in range(3)]
            idx = list(coord)
            for d in order[:phase]:
                idx[d] = slice(None)
            view = hview.at[idx[0], idx[1], idx[2], core, j]
            for r in (1, 3, 2):
                steps = [0, 0, 0]
                steps[order[phase]] = r
                remote(view, view, ag_s, ag_r.at[phase, j], device(*steps, 0)).start()

    def ag_wait(phase, j):
        wait_rows(hidb, 3 * 4 ** phase * (HROWS // SEQ), ag_r.at[phase, j])

    def half(j, off, part):
        order = [(j + k) % 3 for k in range(3)]
        idx = [slice(None)] * 3
        idx[order[2]] = (coord[order[2]] + off) % 4
        idx[order[0]] = slice(2 * part, 2 * part + 2)
        return hview.at[idx[0], idx[1], idx[2], core, j]

    def ag_half(j, off, part, sem, r):
        steps = [0, 0, 0]
        steps[(j + 2) % 3] = r
        view = half(j, off, part)
        remote(view, view, ag_s, ag_r2.at[j, sem], device(*steps, 0)).start()

    HALF = 8 * HROWS // SEQ
    qrows = qbuf.reshape(qbuf.shape[0], LANES)
    lane = lax.broadcasted_iota(jnp.int32, (8, LANES), 1)

    def pack(i, k, carry):
        first = (SHARD * k) // LANES
        off = (SHARD * k) % LANES
        shift = (LANES - off) % LANES
        keep = lane < LANES - off
        for s in range(SEQ):
            base = (s * TILES + first) * DRAFT + i
            lo = qrows[pl.ds(base, 8, stride=2), :]
            hi = qrows[pl.ds(base + 2, 8, stride=2), :]
            lo = pltpu.roll(lo, shift, 1)
            hi = pltpu.roll(hi, shift, 1)
            send[i, pl.ds(pl.multiple_of(k * BLK + s * 8, 8), 8), :] = jnp.where(keep, lo, hi)
        return carry

    mine = pl.ds(pl.multiple_of(me * BLK, 8), BLK)

    def to(i, dev):
        remote(send.at[i, pl.ds(pl.multiple_of(dev * BLK, 8), BLK)], recv.at[i, mine],
               qs, qr_sem.at[i], dev).start()

    def step(d, n):
        return ((coord[d] + n) % 4) * unit[d]

    def class0(i):
        pltpu.make_async_copy(send.at[i, mine], recv.at[i, mine], qr_sem.at[i]).start()
        to(i, partner)

    def class1(i, rc):
        last = core if rc == 0 else 1 - core
        for r in (1, 3, 2):
            for d in range(3):
                steps = [0, 0, 0]
                steps[d] = r
                to(i, device(*steps, rc))

    def class2(i, rc, lo=0, hi=9):
        last = core if rc == 0 else 1 - core

        def body(n, carry):
            a, b = n // 3 + 1, n % 3 + 1
            to(i, step(0, a) + step(1, b) + hop[2][0] + last)
            to(i, hop[0][0] + step(1, a) + step(2, b) + last)
            to(i, step(0, b) + hop[1][0] + step(2, a) + last)
            return carry

        lax.fori_loop(lo, hi, body, 0)

    def class3(i, rc, lo=0, hi=9):
        last = core if rc == 0 else 1 - core

        def body(n, carry):
            a, b = n // 3, n % 3
            for k in range(3):
                to(i, step(0, (a + k) % 3 + 1) + step(1, (b + k) % 3 + 1) + hop[2][k + 1] + last)
            return carry

        lax.fori_loop(lo, hi, body, 0)

    ag_phase(0)
    with scope('qwait'):
        qcp.wait()
    with scope('pack'):
        lax.fori_loop(0, DEV, functools.partial(pack, 0), 0, unroll=16)
    with scope('ex0'):
        class0(0)
        class1(0, 0)
    with scope('ag0'):
        for j in range(3):
            ag_wait(0, j)
    ag_phase(1)
    with scope('ex0a'):
        class1(0, 1)
        class2(0, 0)
    with scope('pack2'):
        lax.fori_loop(0, DEV, functools.partial(pack, 1), 0, unroll=16)
    with scope('ag1'):
        for j in range(3):
            ag_wait(1, j)
    for j in range(3):
        ag_half(j, 0, 0, 0, 1)
        ag_half(j, 0, 1, 1, 3)
    for j in range(3):
        ag_half(j, 0, 1, 2, 1)
        ag_half(j, 0, 0, 2, 3)
    with scope('relay'):
        for j in range(3):
            wait_rows(hidb, HALF, ag_r2.at[j, 0])
            ag_half(j, 3, 0, 2, 1)
            wait_rows(hidb, HALF, ag_r2.at[j, 1])
            ag_half(j, 1, 1, 2, 3)
    with scope('exag2'):
        class0(1)
        class1(1, 0)
        class1(1, 1)
        class2(0, 1)
    d2d = []
    for j in (2, 1, 0):
        with scope(f'ag2_{j}'):
            wait_rows(hidb, 4 * HALF, ag_r2.at[j, 2])
        view = hview.at[:, :, :, core, j]
        cp = remote(view, view, d2d_s, d2d_r.at[j], partner)
        cp.start()
        d2d.append(cp)
    with scope('ex0b'):
        class3(0, 0)
        class3(0, 1)
        class3(1, 0)
    with scope('d2d'):
        for cp in d2d:
            cp.wait_recv()

    def relayout(n, carry):
        def up(b, c):
            x = hidb[pl.ds(pl.multiple_of((48 * n + b) * 48, 16), 48), :]
            bounce[pl.ds(b * PITCH, 48), :] = x.astype(jnp.float32)
            return c

        lax.fori_loop(0, 48, up, 0, unroll=4)
        for g in range(NPOS):
            for u in range(3):
                for kc in range(KC):
                    y = bounce[pl.ds(16 * u * PITCH + g * KC + kc, 16, stride=PITCH), :]
                    hmat[pl.ds(pl.multiple_of(g * BATCH + 48 * n + 16 * u, 16), 16),
                         kc * LANES:(kc + 1) * LANES] = y.astype(jnp.bfloat16)
        return carry

    with scope('relayout'):
        lax.fori_loop(0, 8, relayout, 0)
    wcp.wait()
    tcp.wait()

    z[SHARD:ROWS_P, :] = jnp.full((ROWS_P - SHARD, COLS_P), NEG, jnp.float32)

    def head(n, carry):
        hb = hmat[pl.ds(pl.multiple_of(n * 256, 256), 256), :]
        zt = lax.dot_general(wbuf[...], hb, (((1,), (1,)), ((), ())), preferred_element_type=jnp.float32)
        zt = zt * INV_TEMP
        z[0:SHARD, pl.ds(pl.multiple_of(n * 256, 256), 256)] = zt
        top = jnp.max(zt, axis=0, keepdims=True)
        peak[pl.ds(2 * n, 1), :] = top[:, 0:LANES]
        peak[pl.ds(2 * n + 1, 1), :] = top[:, LANES:]
        return carry

    with scope('head'):
        lax.fori_loop(0, COLS_P // 256, head, 0)

    def local_stats(t, carry):
        cols = pl.ds(pl.multiple_of(t * LANES, LANES), LANES)

        m = peak[pl.ds(t, 1), :]

        def expo(n, s):
            rows = pl.ds(pl.multiple_of(n * 112, 8), 112)
            x = jnp.exp(z[rows, cols] - m)
            z[rows, cols] = x
            return s + jnp.sum(x.reshape(14, 8, LANES), axis=0)

        s8 = lax.fori_loop(0, 9, expo, jnp.zeros((8, LANES), jnp.float32), unroll=3)
        stat[pl.ds(t, 1), :] = m
        stat[pl.ds(CT + t, 1), :] = jnp.sum(s8, axis=0, keepdims=True)
        return carry

    stat[...] = jnp.zeros_like(stat)
    with scope('stats'):
        lax.fori_loop(0, CT, local_stats, 0)
    bcp = pltpu.make_async_copy(z.at[:, DRAFT * BATCH:COLS], bo_hbm, lsem.at[2])
    bcp.start()

    slot, grp = me % 8, me // 8
    near = lambda k: grp * 8 + k
    far = lambda k: k * 8 + slot
    local = stat[0:STAT, :]
    reduce_stage(a1, slot, 8, rs, rr.at[0], near, local)
    with scope('ex1a'):
        class3(1, 1, 0, 8)
    with scope('round1a'):
        parts = finish(a1, 8, rr.at[0])
    reduce_stage(b1, grp, 16, rs, rr.at[1], far, merge_max_sum(parts))
    with scope('ex1b'):
        class3(1, 1, 8, 9)
        class2(1, 1)
        class2(1, 0)
    with scope('round1b'):
        parts = finish(b1, 16, rr.at[1])
    tot = merge_max_sum(parts)
    fac = jnp.exp(local[0:CT] - tot[0:CT]) / tot[CT:2 * CT]
    scale[0:CT, :] = fac
    out_ref[12:16, :] = jnp.concatenate([fac[DRAFT * BT:CT], fac[0:1]], axis=0)

    exrows = exbuf.reshape(exbuf.shape[0], LANES)
    first_id = me * SHARD
    stat[...] = jnp.zeros_like(stat)
    for i in range(DRAFT):
        with scope(f'a2a_{i}'):
            pltpu.make_async_copy(recv.at[i], recv.at[i], qr_sem.at[i]).wait()
        for t in range(BT):
            row = i * BT + t
            sc = scale[row:row + 1, :]
            tok = tok_ref[i:i + 1, t * LANES:(t + 1) * LANES] - first_id
            col0 = i * BATCH + t * LANES

            def block(c, carry, size, valid):
                mass, pp, qp = carry
                q = recv[i, pl.ds(t * LANES * CHUNKS + c, LANES, stride=CHUNKS), :].T
                p = z[pl.ds(pl.multiple_of(c * LANES, LANES), size), col0:col0 + LANES] * sc
                ids = lax.broadcasted_iota(jnp.int32, (size, LANES), 0)
                q = q[0:size]
                if valid < size:
                    q = jnp.where(ids < valid, q, 0.0)
                x = jnp.maximum(p - q, 0.0)
                exrows[pl.ds(c * LANES * 6 + t * 2 + i, valid, stride=6), :] = x[0:valid]
                hit = ids == tok - c * LANES
                fold = lambda v: jnp.sum(v.reshape(size // 8, 8, LANES), axis=0)
                return (mass + fold(x), pp + fold(jnp.where(hit, p, 0.0)), qp + fold(jnp.where(hit, q, 0.0)))

            zero = jnp.zeros((8, LANES), jnp.float32)
            carry = lax.fori_loop(0, CHUNKS - 1, lambda c, v: block(c, v, LANES, LANES), (zero, zero, zero),
                                  unroll=CHUNKS - 1)
            mass, pp, qp = block(CHUNKS - 1, carry, TAIL_P, TAIL)
            stat[row:row + 1, :] = jnp.sum(mass, axis=0, keepdims=True)
            stat[6 + row:7 + row, :] = jnp.sum(pp, axis=0, keepdims=True)
            stat[12 + row:13 + row, :] = jnp.sum(qp, axis=0, keepdims=True)

    ecp = pltpu.make_async_copy(exbuf, ex_hbm, lsem.at[0])
    ecp.start()
    reduce_stage(a2, slot, 8, rs, rr.at[2], near, stat[0:STAT, :])
    with scope('round2a'):
        parts = finish(a2, 8, rr.at[2])
    reduce_stage(b2, grp, 16, rs, rr.at[3], far, merge_add(parts))
    with scope('round2b'):
        parts = finish(b2, 16, rr.at[3])
    tot = merge_add(parts)
    out_ref[0:6, :] = tot[0:6]
    out_ref[6:12, :] = jnp.minimum(tot[6:12] / tot[12:18], 1.0)
    with scope('tail'):
        ecp.wait()
        bcp.wait()
        wait_rows(hidb, 9 * 21 * (HROWS // SEQ), ag_s)
        wait_rows(hidb, DEV // 2 * HROWS, d2d_s)
        wait_rows(send.reshape(DRAFT * DEV * BLK, LANES), DRAFT * (DEV - 1) * BLK, qs)
        wait_rows(qbuf, 2 * (7 + 15) * STAT, rs)


def finish_kernel(ex_ref, bo_ref, stat_ref, res_hbm, bonus_hbm, acc_ref, exp_ref, res, bonus, sems):
    rows = ex_ref.reshape(ex_ref.shape[0], LANES)
    out = res.reshape(res.shape[0], LANES)
    copies = []
    fac = jnp.concatenate([stat_ref[12 + t:13 + t, :] for t in range(BT)], axis=1)
    step = 256
    for n in range(4):
        size = min(step, SHARD - n * step)
        bonus[n * step:n * step + size, :] = bo_ref[n * step:n * step + size, :] * fac
    cp = pltpu.make_async_copy(bonus, bonus_hbm, sems)
    cp.start()
    copies.append(cp)
    mass = jnp.concatenate([stat_ref[i * BT + t:i * BT + t + 1, :] for t in range(BT) for i in range(DRAFT)], axis=0)
    mass = jnp.concatenate([mass] * 4, axis=0)
    for n in range(5):
        def body(k, carry):
            at = pl.ds(pl.multiple_of(n * 1200 + k * 24, 8), 24)
            out[at, :] = rows[at, :] / mass
            return carry

        lax.fori_loop(0, 50, body, 0, unroll=5)
        size = 1200
        if n == 4:
            out[6000:6012, :] = rows[6000:6012, :] / mass[0:12]
            size = 1212
        cp = pltpu.make_async_copy(res.at[pl.ds(n * 1200, size)], res_hbm.at[pl.ds(n * 1200, size)], sems)
        cp.start()
        copies.append(cp)
    acc = stat_ref[6:12, :]
    more = acc[0:BT] * (1.0 + acc[BT:2 * BT])
    for t in range(BT):
        cols = slice(t * LANES, (t + 1) * LANES)
        exp_ref[cols] = more[t]
        for i in range(DRAFT):
            acc_ref[i:i + 1, cols] = acc[i * BT + t:i * BT + t + 1]
    for cp in copies:
        cp.wait()


def verify_local(hid, w_cols, q_rows, draft_tok):
    q = with_layout_constraint(q_rows.reshape(SEQ, DRAFT, TILES, LANES), Layout((0, 2, 1, 3)))
    q = q.transpose(0, 2, 1, 3).reshape(SEQ * TILES * DRAFT, 1, LANES)
    f32 = jnp.float32
    hbm = pl.BlockSpec(memory_space=pl.ANY)
    vmem = pl.BlockSpec(memory_space=pltpu.VMEM)
    dma = pltpu.SemaphoreType.DMA
    ex, bo, st = pl.pallas_call(
        kernel,
        out_shape=[
            jax.ShapeDtypeStruct((SHARD * BT * DRAFT, 1, LANES), f32),
            jax.ShapeDtypeStruct((ROWS_P, BATCH), f32),
            jax.ShapeDtypeStruct((16, LANES), f32),
        ],
        in_specs=[pl.BlockSpec(memory_space=pltpu.HBM)] * 4,
        out_specs=[hbm, hbm, vmem],
        scratch_shapes=[
            pltpu.VMEM((DRAFT, BATCH), jnp.int32),
            pltpu.VMEM((SEQ * TILES * DRAFT + 20, 1, LANES), f32),
            pltpu.VMEM((SHARD, DIM), jnp.bfloat16),
            pltpu.VMEM((SEQ, NPOS, DIM), jnp.bfloat16),
            pltpu.VMEM((DEV * HROWS, LANES), jnp.bfloat16),
            pltpu.VMEM((48 * PITCH, LANES), f32),
            pltpu.VMEM((COLS_P, DIM), jnp.bfloat16),
            pltpu.VMEM((ROWS_P, COLS_P), f32),
            pltpu.VMEM((DRAFT, DEV * BLK, LANES), f32),
            pltpu.VMEM((DRAFT, DEV * BLK, LANES), f32),
            pltpu.VMEM((SHARD * BT * DRAFT, 1, LANES), f32),
            pltpu.VMEM((24, LANES), f32),
            pltpu.VMEM((16, LANES), f32),
            pltpu.VMEM((16, LANES), f32),
            pltpu.VMEM((8 * STAT, 1, LANES), f32),
            pltpu.VMEM((16 * STAT, 1, LANES), f32),
            pltpu.VMEM((8 * STAT, 1, LANES), f32),
            pltpu.VMEM((16 * STAT, 1, LANES), f32),
            dma((4,)),
            dma, dma((2, 3)), dma((3, 3)), dma, dma((3,)), dma, dma((2,)), dma, dma((4,)),
        ],
        compiler_params=pltpu.CompilerParams(vmem_limit_bytes=40 * 2 ** 20, has_side_effects=True, collective_id=0),
    )(*(pltpu.with_memory_space_constraint(x, pltpu.HBM) for x in (q, w_cols.T, hid, draft_tok.T)))
    res, bonus, acc, expected = pl.pallas_call(
        finish_kernel,
        out_shape=[
            jax.ShapeDtypeStruct((SHARD * BT * DRAFT, 1, LANES), f32),
            jax.ShapeDtypeStruct((SHARD, BATCH), f32),
            jax.ShapeDtypeStruct((DRAFT, BATCH), f32),
            jax.ShapeDtypeStruct((BATCH,), f32),
        ],
        in_specs=[vmem] * 3,
        out_specs=[hbm, hbm, vmem, vmem],
        scratch_shapes=[
            pltpu.VMEM((SHARD * BT * DRAFT, 1, LANES), f32),
            pltpu.VMEM((SHARD, BATCH), f32),
            dma,
        ],
        compiler_params=pltpu.CompilerParams(vmem_limit_bytes=12 * 2 ** 20),
    )(ex, bo, st)
    res = with_layout_constraint(res.reshape(SHARD, BT, DRAFT, LANES).transpose(0, 2, 1, 3), Layout((0, 2, 1, 3)))
    residual = res.reshape(SHARD, DRAFT, BATCH).transpose(2, 1, 0)
    return acc.T, expected, residual, bonus.T


def solution(mesh):
    return jax.shard_map(
        verify_local,
        mesh=mesh,
        in_specs=(P(('dp', 'tp'), None, None), P(None, 'tp'), P(('dp', 'tp'), None, None), P('dp', None)),
        out_specs=(P('dp', None), P('dp'), P('dp', None, 'tp'), P('dp', 'tp')),
        check_vma=False,
    )
```

profile of v0, /device:TPU:1, one launch (start us, length us, event | category | flops | bytes accessed | tf_op | source)
XLA Modules:
  0.0 73.3 jit_solution(10048937306396593672)
XLA Ops:
  0.6 69.8 %shard_map.75 = (f32[6012,1,128]{2,1,0:T(1,128)S(1)}, f32[1008,384]{1,0:T(8,128)S(1)}, f32[16,128]{1,0:T(8,128)S(1)}) custom-call(f32[6012,1,128]{2,1,0:T(1,128)} %bitcast.17, bf16[1002,2048]{1,0:T(8,128)(2,1)} %bitcast.16, bf16[3,3,2048]{2,1,0:T(4,128)(2,1)} %h_hbm.1, s32[2,384]{1,0:T(2,128)} %bitcast.18), custom_call_target="tpu_custom_call" | custom-call | tf_op jit(solution)/shard_map/pallas_call | solution.py:447
  70.5 2.8 %shard_map.76 = (f32[6012,1,128]{2,1,0:T(1,128)}, f32[1002,384]{1,0:T(8,128)}, f32[2,384]{1,0:T(2,128)}, f32[384]{0:T(512)}) custom-call(f32[6012,1,128]{2,1,0:T(1,128)S(1)} %get-tuple-element.11.ex_ref, f32[1008,384]{1,0:T(8,128)S(1)} %get-tuple-element.12.bo_ref, f32[16,128]{1,0:T(8,128)S(1)} %get-tuple-element.13.stat_ref), custom_call_target="tpu_custom_call" | custom-call | tf_op jit(solution)/shard_map/pallas_call | solution.py:480
where the time goes:
time: 73.5 us; the launch traced here: 73.3 us
  Pallas kernels  72.6 us (99%)
    pallas_call x1, Pallas kernels, verify_local(): pl.pallas_call(kernel, out_shape=[jax.ShapeDtypeStruct((SHARD * BT * DRAF...  69.8 us
    pallas_call x1, Pallas kernels, verify_local(): pl.pallas_call(finish_kernel, out_shape=[jax.ShapeDtypeStruct((SHARD * BT...  2.83 us

commit v1 on v0

--- a/solution.py
+++ b/solution.py
@@ -250,6 +250,7 @@
         class1(1, 0)
         class1(1, 1)
         class2(0, 1)
+        class3(0, 0, 0, 5)
     d2d = []
     for j in (2, 1, 0):
         with scope(f'ag2_{j}'):
@@ -259,9 +260,10 @@
         cp.start()
         d2d.append(cp)
     with scope('ex0b'):
-        class3(0, 0)
+        class3(0, 0, 5, 9)
         class3(0, 1)
         class3(1, 0)
+        class3(1, 1, 0, 4)
     with scope('d2d'):
         for cp in d2d:
             cp.wait_recv()
@@ -329,13 +331,13 @@
     local = stat[0:STAT, :]
     reduce_stage(a1, slot, 8, rs, rr.at[0], near, local)
     with scope('ex1a'):
-        class3(1, 1, 0, 8)
+        class3(1, 1, 4, 9)
+        class2(1, 1, 0, 3)
     with scope('round1a'):
         parts = finish(a1, 8, rr.at[0])
     reduce_stage(b1, grp, 16, rs, rr.at[1], far, merge_max_sum(parts))
     with scope('ex1b'):
-        class3(1, 1, 8, 9)
-        class2(1, 1)
+        class2(1, 1, 3, 9)
         class2(1, 0)
     with scope('round1b'):
         parts = finish(b1, 16, rr.at[1])

time: 73.5 us -> 72.2 us (0.982)
  Pallas kernels: 72.6 us -> 71.5 us
    pallas_call x1, Pallas kernels: 69.8 us -> 68.6 us  [verify_local(): pl.pallas_call(kernel, out_shape=[jax.ShapeDtypeStruct((SHARD * BT * DRAF...]
where the time goes in v1:
time: 72.2 us; the launch traced here: 72.1 us
  Pallas kernels  71.5 us (99%)
    pallas_call x1, Pallas kernels, verify_local(): pl.pallas_call(kernel, out_shape=[jax.ShapeDtypeStruct((SHARD * BT * DRAF...  68.6 us
    pallas_call x1, Pallas kernels, verify_local(): pl.pallas_call(finish_kernel, out_shape=[jax.ShapeDtypeStruct((SHARD * BT...  2.83 us

profile of v1, /device:TPU:1, one launch (start us, length us, event | category | flops | bytes accessed | tf_op | source)
XLA Modules:
  0.0 72.1 jit_solution(6555814172197851965)
XLA Ops:
  0.6 68.6 %shard_map.75 = (f32[6012,1,128]{2,1,0:T(1,128)S(1)}, f32[1008,384]{1,0:T(8,128)S(1)}, f32[16,128]{1,0:T(8,128)S(1)}) custom-call(f32[6012,1,128]{2,1,0:T(1,128)} %bitcast.17, bf16[1002,2048]{1,0:T(8,128)(2,1)} %bitcast.16, bf16[3,3,2048]{2,1,0:T(4,128)(2,1)} %h_hbm.1, s32[2,384]{1,0:T(2,128)} %bitcast.18), custom_call_target="tpu_custom_call" | custom-call | tf_op jit(solution)/shard_map/pallas_call | solution.py:449
  69.3 2.8 %shard_map.76 = (f32[6012,1,128]{2,1,0:T(1,128)}, f32[1002,384]{1,0:T(8,128)}, f32[2,384]{1,0:T(2,128)}, f32[384]{0:T(512)}) custom-call(f32[6012,1,128]{2,1,0:T(1,128)S(1)} %get-tuple-element.11.ex_ref, f32[1008,384]{1,0:T(8,128)S(1)} %get-tuple-element.12.bo_ref, f32[16,128]{1,0:T(8,128)S(1)} %get-tuple-element.13.stat_ref), custom_call_target="tpu_custom_call" | custom-call | tf_op jit(solution)/shard_map/pallas_call | solution.py:482

commit v2 on v1

--- a/solution.py
+++ b/solution.py
@@ -250,7 +250,7 @@
         class1(1, 0)
         class1(1, 1)
         class2(0, 1)
-        class3(0, 0, 0, 5)
+        class3(0, 0)
     d2d = []
     for j in (2, 1, 0):
         with scope(f'ag2_{j}'):
@@ -260,7 +260,6 @@
         cp.start()
         d2d.append(cp)
     with scope('ex0b'):
-        class3(0, 0, 5, 9)
         class3(0, 1)
         class3(1, 0)
         class3(1, 1, 0, 4)

time: 72.2 us -> 72.1 us (level)
  no operation moved by 1% of the time
where the time goes in v2:
time: 72.1 us; the launch traced here: 72 us
  Pallas kernels  71.3 us (99%)
    pallas_call x1, Pallas kernels, verify_local(): pl.pallas_call(kernel, out_shape=[jax.ShapeDtypeStruct((SHARD * BT * DRAF...  68.5 us
    pallas_call x1, Pallas kernels, verify_local(): pl.pallas_call(finish_kernel, out_shape=[jax.ShapeDtypeStruct((SHARD * BT...  2.83 us

profile of v2, /device:TPU:1, one launch (start us, length us, event | category | flops | bytes accessed | tf_op | source)
XLA Modules:
  0.0 72.0 jit_solution(13502573058198126226)
XLA Ops:
  0.6 68.5 %shard_map.75 = (f32[6012,1,128]{2,1,0:T(1,128)S(1)}, f32[1008,384]{1,0:T(8,128)S(1)}, f32[16,128]{1,0:T(8,128)S(1)}) custom-call(f32[6012,1,128]{2,1,0:T(1,128)} %bitcast.17, bf16[1002,2048]{1,0:T(8,128)(2,1)} %bitcast.16, bf16[3,3,2048]{2,1,0:T(4,128)(2,1)} %h_hbm.1, s32[2,384]{1,0:T(2,128)} %bitcast.18), custom_call_target="tpu_custom_call" | custom-call | tf_op jit(solution)/shard_map/pallas_call | solution.py:448
  69.1 2.8 %shard_map.76 = (f32[6012,1,128]{2,1,0:T(1,128)}, f32[1002,384]{1,0:T(8,128)}, f32[2,384]{1,0:T(2,128)}, f32[384]{0:T(512)}) custom-call(f32[6012,1,128]{2,1,0:T(1,128)S(1)} %get-tuple-element.11.ex_ref, f32[1008,384]{1,0:T(8,128)S(1)} %get-tuple-element.12.bo_ref, f32[16,128]{1,0:T(8,128)S(1)} %get-tuple-element.13.stat_ref), custom_call_target="tpu_custom_call" | custom-call | tf_op jit(solution)/shard_map/pallas_call | solution.py:481
